TPU v7x, 32 devices: a whole 2x2x4 slice. The times are simulated.
32 devices in a mesh: grp: 2 (over x), tok: 8 (over z, y), mdl: 2 (over core).
Axes of the slice: x: 2, y: 2, z: 4, core: 2. Of those that a mesh axis runs over, the one named last changes fastest.
Arguments:
- hidden: bfloat16 [1024, 4096], P(('grp', 'tok'), 'mdl'), parts along dimension 0, may hold values from -3 to 3
- queries: bfloat16 [1024, 16, 128], P(('grp', 'tok'), 'mdl'), parts along dimension 0, may hold values from -8 to 8
- cache: bfloat16 [16, 2048, 4, 2, 128], P(('grp', 'tok'), None, 'mdl'), parts along dimension 0, may hold values from -8 to 8
- cache_lengths: int32 [16], P(('grp', 'tok')), parts along dimension 0, may hold values from 128 to 2048, as said below
- wkv: bfloat16 [4096, 4, 2, 128], P('tok', 'mdl'), may hold values from -0.09375 to 0.09375
- wo: bfloat16 [16, 128, 4096], P('mdl', None, 'tok'), may hold values from -0.5 to 0.5
- attn_gain: bfloat16 [4096], replicated, may hold values from 0.5 to 1.5
- moe_gain: bfloat16 [4096], replicated, may hold values from 0.5 to 1.5
- w_gate: bfloat16 [16, 4096, 1792], P(('tok', 'mdl')), may hold values from -0.09375 to 0.09375
- w_up: bfloat16 [16, 4096, 1792], P(('tok', 'mdl')), may hold values from -0.09375 to 0.09375
- w_down: bfloat16 [16, 1792, 4096], P(('tok', 'mdl')), may hold values from -0.0625 to 0.0625
- expert_ids: int32 [1024, 2], P(('grp', 'tok', 'mdl')), parts along dimension 0, may hold values from 0 to 3, all different within a row; in each aligned block of 32 rows (0 to 31, 32 to 63, ...) at most 18 rows name the same one
- gates: float32 [1024, 2], P(('grp', 'tok', 'mdl')), parts along dimension 0, may hold values from 0.1 to 1
Outputs:
- mixed: bfloat16 [1024, 4096], P(('grp', 'tok', 'mdl')), parts along dimension 0
- fresh_key_value: bfloat16 [1024, 4, 2, 128], P(('grp', 'tok'), 'mdl'), parts along dimension 0
There are 2 independent parts, one for each index of `grp`. A program takes and returns all parts, laid end to end along the dimension named above; an argument that names none is the same for every part. Nothing has to cross between parts.
Inputs may be any that keep to these rules, and one draw needn't show every extreme that they name: `expert_ids`: each token names 2 different experts; in aligned blocks of 32 rows no expert is named by more than 18 rows, a bound that some block reaches. `cache_lengths`: some rollout holds exactly 2048 cached positions.
All inputs are finite; a program needn't handle non-finite values.
Results may differ from a plain program's by a relative error of at most 0.007.
Values may be sent and summed in bfloat16 or wider, within the bound.
A program may use at most 128 MiB of HBM per device.

v0:
```python
import math
import jax
import jax.numpy as jnp
from jax import lax
from jax.sharding import PartitionSpec as P

EXPERTS = 4
TOPK = 2
eps_norm = 1e-05
rope_base = 1000000.0
mask_fill = -1e30


def rms_scale(values_in, gain):
    values = values_in.astype(jnp.float32)
    meansq = jnp.mean(values * values, axis=-1, keepdims=True)
    return values * lax.rsqrt(meansq + eps_norm) * gain.astype(jnp.float32)


def rotate(key_rows, positions):
    half_dim = key_rows.shape[-1] // 2
    inverse = jnp.exp(
        jnp.arange(half_dim, dtype=jnp.float32) * (-2.0 * math.log(rope_base) / key_rows.shape[-1])
    )
    angle = positions.astype(jnp.float32)[:, None] * inverse[None, :]
    cosine = jnp.cos(angle)[:, None, :]
    sine_vals = jnp.sin(angle)[:, None, :]
    front_half = key_rows[..., :half_dim]
    back_half = key_rows[..., half_dim:]
    return jnp.concatenate(
        [front_half * cosine - back_half * sine_vals, back_half * cosine + front_half * sine_vals],
        axis=-1,
    )


def score_rows(query_rows, key_rows, scale_factor):
    return (
        lax.dot_general(
            query_rows, key_rows, (((1,), (1,)), ((), ())), preferred_element_type=jnp.float32
        )
        * scale_factor
    )


def head_attention(query_rows, cache_keys, cache_values, length, new_keys, new_values, head_group):
    row_count = query_rows.shape[0]
    block_len = min(512, cache_keys.shape[0])
    scale_factor = 1.0 / math.sqrt(query_rows.shape[1])
    token_of_row = jnp.arange(row_count) // head_group
    block_total = (length + block_len - 1) // block_len

    def block_scores(block_idx):
        row_offset = block_idx * block_len
        block_keys = lax.dynamic_slice_in_dim(cache_keys, row_offset, block_len, 0)
        allowed = row_offset + jnp.arange(block_len) < length
        return (
            jnp.where(
                allowed[None, :], score_rows(query_rows, block_keys, scale_factor), mask_fill
            ),
            allowed,
        )

    new_allowed = jnp.arange(new_keys.shape[0])[None, :] <= token_of_row[:, None]
    new_scores = jnp.where(new_allowed, score_rows(query_rows, new_keys, scale_factor), mask_fill)
    first_max = jnp.max(new_scores, axis=1)
    first_sum = jnp.sum(
        jnp.where(new_allowed, jnp.exp(new_scores - first_max[:, None]), 0.0), axis=1
    )

    def first_pass(block_idx, carry):
        run_max, run_sum = carry
        scores, allowed = block_scores(block_idx)
        next_max = jnp.maximum(run_max, jnp.max(scores, axis=1))
        weights = jnp.where(allowed[None, :], jnp.exp(scores - next_max[:, None]), 0.0)
        return (next_max, run_sum * jnp.exp(run_max - next_max) + jnp.sum(weights, axis=1))

    row_max, row_sum = lax.fori_loop(0, block_total, first_pass, (first_max, first_sum))
    new_probs = (
        jnp.where(new_allowed, jnp.exp(new_scores - row_max[:, None]), 0.0) / row_sum[:, None]
    ).astype(jnp.bfloat16)
    start_total = jnp.dot(new_probs, new_values, preferred_element_type=jnp.float32)

    def second_pass(block_idx, total):
        scores, allowed = block_scores(block_idx)
        probs = (
            jnp.where(allowed[None, :], jnp.exp(scores - row_max[:, None]), 0.0) / row_sum[:, None]
        ).astype(jnp.bfloat16)
        block_values = lax.dynamic_slice_in_dim(cache_values, block_idx * block_len, block_len, 0)
        return total + jnp.dot(probs, block_values, preferred_element_type=jnp.float32)

    total = lax.fori_loop(0, block_total, second_pass, start_total)
    return total.astype(jnp.bfloat16)


def shards(
    hidden,
    queries,
    cache,
    cache_lengths,
    wkv,
    wo,
    attn_gain,
    moe_gain,
    w_gate,
    w_up,
    w_down,
    expert_ids,
    gates,
):
    full_rows = lax.all_gather(hidden, "mdl", axis=1, tiled=True)
    span_len = full_rows.shape[0]
    normalized_input = rms_scale(full_rows, attn_gain).astype(jnp.bfloat16)
    kv_heads = wkv.shape[1]
    head_dim = wkv.shape[3]
    weight_piece = lax.all_gather(wkv, "tok", axis=0, tiled=True)
    key_value_projection = jnp.dot(
        normalized_input,
        weight_piece.reshape(weight_piece.shape[0], -1),
        preferred_element_type=jnp.float32,
    ).reshape(span_len, kv_heads, 2, head_dim)
    length = cache_lengths[0]
    positions = length + jnp.arange(span_len, dtype=jnp.int32)
    fresh_key_value = jnp.stack(
        [rotate(key_value_projection[:, :, 0], positions), key_value_projection[:, :, 1]], axis=2
    ).astype(jnp.bfloat16)
    head_group = queries.shape[1] // kv_heads
    outputs = []
    for head_index in range(kv_heads):
        query_rows = queries[:, head_index * head_group : (head_index + 1) * head_group].reshape(
            span_len * head_group, head_dim
        )
        attended = head_attention(
            query_rows,
            cache[0, :, head_index, 0],
            cache[0, :, head_index, 1],
            length,
            fresh_key_value[:, head_index, 0],
            fresh_key_value[:, head_index, 1],
            head_group,
        )
        outputs.append(attended.reshape(span_len, head_group * head_dim))
    heads_out = jnp.concatenate(outputs, axis=1)
    weight_piece = lax.all_gather(wo, "tok", axis=2, tiled=True)
    attn_out = jnp.dot(
        heads_out,
        weight_piece.reshape(-1, weight_piece.shape[2]),
        preferred_element_type=jnp.float32,
    )
    core_rows = span_len // lax.axis_size("mdl")
    core_start = lax.axis_index("mdl") * core_rows
    summed_heads = lax.psum(attn_out, "mdl")
    attn_rows = lax.dynamic_slice_in_dim(summed_heads, core_start, core_rows, 0)
    resid = (
        lax.dynamic_slice_in_dim(full_rows, core_start, core_rows, 0).astype(jnp.float32)
        + attn_rows
    )
    moe_in = rms_scale(resid, moe_gain).astype(jnp.bfloat16)
    expert_range = jnp.arange(EXPERTS)
    matches = expert_ids[:, :, None] == expert_range[None, None, :]
    chosen = jnp.sum(matches.astype(jnp.int32), axis=1)
    route = jnp.sum(jnp.where(matches, gates[:, :, None], 0.0), axis=1)
    slot_of = jnp.cumsum(chosen, axis=0) - chosen
    capacity = core_rows * TOPK * 9 // (8 * EXPERTS)
    slot_range = jnp.arange(capacity)
    select = (slot_of.T[:, None, :] == slot_range[None, :, None]) & (chosen.T[:, None, :] > 0)
    send_rows = jnp.einsum(
        "eci,id->ecd", select.astype(jnp.bfloat16), moe_in, preferred_element_type=jnp.float32
    ).astype(jnp.bfloat16)
    owners = lax.axis_size("tok") * lax.axis_size("mdl")
    slabs = owners // EXPERTS
    model_width = moe_in.shape[1]
    core_count = lax.axis_size("mdl")
    send_chip = jnp.repeat(send_rows, slabs // core_count, axis=0)
    received = lax.all_to_all(send_chip, "tok", split_axis=0, concat_axis=0, tiled=True)
    chip_count = received.shape[0]
    item_count = received.shape[1]
    both_cores = lax.all_gather(received[:, None], "mdl", axis=1, tiled=True)
    received = both_cores.reshape(-1, item_count, model_width)
    flat_rows = received.reshape(-1, model_width)
    gate_val = jnp.dot(flat_rows, w_gate[0], preferred_element_type=jnp.float32)
    up_val = jnp.dot(flat_rows, w_up[0], preferred_element_type=jnp.float32)
    slab_hidden = (jax.nn.silu(gate_val) * up_val).astype(jnp.bfloat16)
    slab_out = jnp.dot(slab_hidden, w_down[0], preferred_element_type=jnp.float32).astype(
        jnp.bfloat16
    )
    slab_out = slab_out.reshape(received.shape)
    per_core = slab_out.reshape(chip_count, core_count, item_count, model_width).astype(jnp.float32)
    chip_total = lax.psum_scatter(
        per_core.astype(jnp.bfloat16), "mdl", scatter_dimension=1, tiled=True
    ).astype(jnp.float32)
    returned = lax.all_to_all(
        chip_total[:, 0].astype(jnp.bfloat16), "tok", split_axis=0, concat_axis=0, tiled=True
    ).astype(jnp.float32)
    summed = jnp.sum(returned.reshape(EXPERTS, slabs // core_count, capacity, model_width), axis=1)
    weight_table = select.astype(jnp.float32) * route.T[:, None, :]
    moe_out = jnp.einsum("eci,ecd->id", weight_table, summed, precision=lax.Precision.HIGHEST)
    mixed = (resid + moe_out).astype(jnp.bfloat16)
    return (mixed, fresh_key_value)


def solution(mesh):
    in_specs = (
        P(("grp", "tok"), "mdl"),
        P(("grp", "tok"), "mdl", None),
        P(("grp", "tok"), None, "mdl", None, None),
        P(("grp", "tok")),
        P("tok", "mdl", None, None),
        P("mdl", None, "tok"),
        P(),
        P(),
        P(("tok", "mdl"), None, None),
        P(("tok", "mdl"), None, None),
        P(("tok", "mdl"), None, None),
        P(("grp", "tok", "mdl"), None),
        P(("grp", "tok", "mdl"), None),
    )
    out_specs = (P(("grp", "tok", "mdl"), None), P(("grp", "tok"), "mdl", None, None))
    return jax.shard_map(shards, mesh=mesh, in_specs=in_specs, out_specs=out_specs, check_vma=False)
```

profile of v0, /device:TPU:0, one launch (start us, length us, event | category | flops | bytes accessed | tf_op | source)
XLA Modules:
  0.0 394.5 jit_solution(5354055071857114779)
XLA Ops:
  7.2 0.7 all-gather.5.cloned.1.call-update
  8.0 0.7 all-gather.7.cloned.1.call-update
  8.7 0.0 all-reduce.2.cloned.1.call-start
  9.4 0.7 convert_element_type.71
  10.1 2.5 all_gather.12
  12.6 0.2 fusion.73
  12.8 0.2 multiply_cosine_fusion
  13.1 3.0 fusion.115
  16.1 0.1 copy_bitcast_fusion.2
  16.2 0.1 copy_bitcast_fusion
  16.4 69.3 %all-gather.5.cloned.1.call-done = bf16[4096,2,2,128]{3,2,1,0:T(2,128)(2,1)} async-done(((bf16[512,2,2,128]{3,2,1,0:T(2,128)(2,1)}), bf16[4096,2,2,128]{3,2,1,0:T(2,128)(2,1)}) %all-gather.5.cloned.1.call-update) | async-done | bytes 4194320 | tf_op jit(solution)/shard_map/all_gather | solution.py:115
  85.7 11.3 %copy.85 = bf16[4096,2,2,128]{0,3,2,1:T(8,128)(2,1)} copy(bf16[4096,2,2,128]{3,2,1,0:T(2,128)(2,1)} %all-gather.5.cloned.1.call-done) | data formatting | bytes 8388608 | tf_op jit(solution)/shard_map/reshape | solution.py:118
  97.0 3.7 fusion.119
  100.6 0.1 subtract_convert_fusion
  100.7 0.1 maximum_bitcast_fusion
  100.8 0.2 fusion.118
  101.0 0.2 fusion.117
  101.2 0.1 select_reduce_fusion.3
  101.2 1.1 while.44
  101.3 0.7 add_compare_fusion.8
  101.9 0.3 fusion.144
  102.2 0.2 select_reduce_fusion.7
  102.4 0.2 fusion.92
  102.6 1.2 while.45
  102.6 0.7 add_compare_fusion.9
  103.3 0.5 fusion.148
  103.9 0.1 reshape.162
  103.9 1.1 while.46
  103.9 0.7 add_compare_fusion.10
  104.6 0.3 fusion.150
  104.9 0.2 select_reduce_fusion.8
  105.1 0.2 fusion.93
  105.3 1.2 while.47
  105.3 0.7 add_compare_fusion.11
  106.0 0.5 fusion.154
  106.5 0.1 reshape.164
  106.6 104.6 %all-gather.7.cloned.1.call-done = bf16[8,128,4096]{2,1,0:T(8,128)(2,1)} async-done(((bf16[8,128,512]{2,1,0:T(8,128)(2,1)}), bf16[8,128,4096]{2,1,0:T(8,128)(2,1)}) %all-gather.7.cloned.1.call-update) | async-done | bytes 8388624 | tf_op jit(solution)/shard_map/all_gather | solution.py:143
  211.2 6.1 %fusion.84 = f32[64,4096]{1,0:T(8,128)} fusion(bf16[1024,4096]{1,0:T(8,128)(2,1)} %bitcast.113, bf16[64,512]{1,0:T(8,128)(2,1)S(1)} %reshape.164, bf16[64,512]{1,0:T(8,128)(2,1)S(1)} %reshape.162), kind=kOutput, calls=%fused_computation.98 | convolution fusion | flops 537133056 | bytes 9568256 | tf_op jit(solution)/shard_map/dot_general | solution.py:144
  217.3 0.0 all-gather.9.cloned.1.call-start
  217.4 0.1 copy.74
  217.5 0.1 reduce_window_sum.11
  217.6 0.1 copy.76
  217.7 17.4 %all-reduce.2.cloned.1.call-done = f32[64,4096]{1,0:T(8,128)} async-done(((f32[64,4096]{1,0:T(8,128)}), f32[64,4096]{1,0:T(8,128)}) %all-reduce.2.cloned.1.call-update) | async-done | bytes 1048592 | tf_op jit(solution)/shard_map/psum | solution.py:151
  235.1 1.2 multiply_reduce_fusion
  236.3 1.5 convolution_convert_fusion
  237.8 0.2 broadcast_in_dim.140
  238.0 43.0 %all_to_all.10 = bf16[8,18,4096]{2,1,0:T(8,128)(2,1)S(1)} all-to-all(bf16[8,18,4096]{2,1,0:T(8,128)(2,1)S(1)} %bitcast.114), channel_id=1, replica_groups=mesh['grp'=2,'tok'=8,'mdl'=2] {'tok'}, dimensions={0} | all-to-all | bytes 2359296 | tf_op jit(solution)/shard_map/all_to_all | solution.py:174
  281.0 1.7 copy.77
  282.7 0.2 reduce-scatter.2.cloned.1.call-start
  282.9 9.9 %all-gather.9.cloned.1.call-done = bf16[8,36,4096]{2,0,1:T(8,128)(2,1)} async-done(((bf16[8,18,4096]{2,0,1:T(8,128)(2,1)}), bf16[8,36,4096]{2,0,1:T(8,128)(2,1)}) %all-gather.9.cloned.1.call-update) | async-done | bytes 2359312 | tf_op jit(solution)/shard_map/all_gather | solution.py:177
  292.8 3.0 copy.78
  295.8 2.1 reshape_reshape.6
  297.9 9.1 %fusion.54 = f32[288,1792]{1,0:T(8,128)S(1)} fusion(bf16[288,4096]{1,0:T(8,128)(2,1)} %reshape_reshape.6, bf16[1,4096,1792]{2,1,0:T(8,128)(2,1)} %param.29), kind=kOutput, calls=%fused_computation.62 | convolution fusion | flops 4227858432 | bytes 19103744 | tf_op jit(solution)/shard_map/dot_general | solution.py:180
  307.1 9.9 %fusion.66 = bf16[288,1792]{1,0:T(8,128)(2,1)S(1)} fusion(bf16[288,4096]{1,0:T(8,128)(2,1)S(1)} %copy-done.4, bf16[1,4096,1792]{2,1,0:T(8,128)(2,1)} %param.30, f32[288,1792]{1,0:T(8,128)S(1)} %fusion.54), kind=kOutput, calls=%fused_computation.73 | convolution fusion | flops 4230955008 | bytes 20135936 | tf_op jit(solution)/shard_map/dot_general | solution.py:181
  317.0 5.7 %fusion.56 = bf16[288,4096]{1,0:T(8,128)(2,1)} fusion(bf16[288,1792]{1,0:T(8,128)(2,1)S(1)} %fusion.66, bf16[1,1792,4096]{2,1,0:T(8,128)(2,1)S(1)} %bitcast.122), kind=kOutput, calls=%fused_computation.64 | convolution fusion | flops 4229038080 | bytes 18071552 | tf_op jit(solution)/shard_map/dot_general | solution.py:183
  322.7 2.7 reshape_reshape.7
  325.5 2.7 copy.79
  328.2 11.4 %reduce-scatter.2.cloned.1.call-done = bf16[8,1,18,4096]{3,0,2,1:T(8,128)(2,1)} async-done(((bf16[8,2,18,4096]{3,0,2,1:T(8,128)(2,1)}), bf16[8,1,18,4096]{3,0,2,1:T(8,128)(2,1)}) %reduce-scatter.2.cloned.1.call-update) | async-done | bytes 1179664 | tf_op jit(solution)/shard_map/reduce_scatter | solution.py:188
  339.6 3.2 copy.80
  342.8 5.9 %all-to-all-start.1 = ((bf16[8,18,4096]{2,1,0:T(8,128)(2,1)}), bf16[8,18,4096]{2,1,0:T(8,128)(2,1)S(1)}, u32[]{:S(2)}, u32[]{:S(2)}) async-start(bf16[8,18,4096]{2,1,0:T(8,128)(2,1)} %copy.80), calls=%async_computation.2 | async-start | bytes 3145728 | tf_op jit(solution)/shard_map/all_to_all | solution.py:191
  348.8 0.7 copy.83
  349.5 36.6 %all-to-all-done.1 = bf16[8,18,4096]{2,1,0:T(8,128)(2,1)S(1)} async-done(((bf16[8,18,4096]{2,1,0:T(8,128)(2,1)}), bf16[8,18,4096]{2,1,0:T(8,128)(2,1)S(1)}, u32[]{:S(2)}, u32[]{:S(2)}) %all-to-all-start.1) | async-done | bytes 1179680 | tf_op jit(solution)/shard_map/all_to_all | solution.py:191
  386.0 0.3 convert_reduce_fusion
  386.3 1.6 fusion.60
  (54 shorter events, 0.4 us)
Async XLA Ops:
  7.2 5.9 %copy-start.5 = (bf16[64,8,128]{2,1,0:T(8,128)(2,1)S(1)}, bf16[64,8,128]{2,1,0:T(8,128)(2,1)}, u32[]{:S(2)}) copy-start(bf16[64,8,128]{2,1,0:T(8,128)(2,1)} %param.22) | copy-start | bytes 393220
  7.2 5.9 %copy-start.2 = (bf16[1,2048,2,2,128]{4,3,2,1,0:T(2,128)(2,1)S(1)}, bf16[1,2048,2,2,128]{4,3,2,1,0:T(2,128)(2,1)}, u32[]{:S(2)}) copy-start(bf16[1,2048,2,2,128]{4,3,2,1,0:T(2,128)(2,1)} %param.23) | copy-start | bytes 6291460
  7.2 78.5 %all-gather.5.cloned.1.call-start = ((), (), s32[]{:S(2)}) async-start(), calls=%async_computation.3 | async-start | bytes 4718592 | tf_op jit(solution)/shard_map/all_gather | solution.py:115
  7.9 203.3 %all-gather.7.cloned.1.call-start = ((), (), s32[]{:S(2)}) async-start(), calls=%async_computation.4 | async-start | bytes 9437184 | tf_op jit(solution)/shard_map/all_gather | solution.py:143
  8.7 226.4 %all-reduce.2.cloned.1.call-start = ((), (), s32[]{:S(2)}) async-start(), calls=%async_computation.5 | async-start | bytes 2097152 | tf_op jit(solution)/shard_map/psum | solution.py:151
  12.6 223.7 %copy-start = (bf16[64,4096]{1,0:T(8,128)(2,1)}, bf16[64,4096]{1,0:T(8,128)(2,1)S(1)}, u32[]{:S(2)}) copy-start(bf16[64,4096]{1,0:T(8,128)(2,1)S(1)} %all_gather.12) | copy-start | bytes 1572868
  211.2 6.2 %copy-start.7 = (s32[32,2]{0,1:T(2,128)S(1)}, s32[32,2]{0,1:T(2,128)}, u32[]{:S(2)}) copy-start(s32[32,2]{0,1:T(2,128)} %param.32) | copy-start | bytes 772
  211.2 6.4 %copy-start.6 = (bf16[4096]{0:T(1024)(128)(2,1)S(1)}, bf16[4096]{0:T(1024)(128)(2,1)}, u32[]{:S(2)}) copy-start(bf16[4096]{0:T(1024)(128)(2,1)} %param.28) | copy-start | bytes 24580
  217.3 75.5 %all-gather.9.cloned.1.call-start = ((), (), s32[]{:S(2)}) async-start(), calls=%async_computation.7 | async-start | bytes 3538944 | tf_op jit(solution)/shard_map/all_gather | solution.py:177
  282.7 57.0 %reduce-scatter.2.cloned.1.call-start = ((), (), s32[]{:S(2)}) async-start(), calls=%async_computation.6 | async-start | bytes 3538944 | tf_op jit(solution)/shard_map/reduce_scatter | solution.py:188
  297.9 9.1 %copy-start.4 = (bf16[288,4096]{1,0:T(8,128)(2,1)S(1)}, bf16[288,4096]{1,0:T(8,128)(2,1)}, u32[]{:S(2)}) copy-start(bf16[288,4096]{1,0:T(8,128)(2,1)} %reshape_reshape.6) | copy-start | bytes 7077892
  297.9 19.0 %slice-start = ((s8[14680064]{0:T(1024)(128)(4,1)}), s8[4194304]{0:T(1024)(128)(4,1)S(1)}, s32[]{:S(2)}) async-start(s8[14680064]{0:T(1024)(128)(4,1)} %bitcast.121), calls=%async_computation.8 | async-start | bytes 8388608
  297.9 19.0 %slice-start.1 = ((s8[14680064]{0:T(1024)(128)(4,1)}), s8[4194304]{0:T(1024)(128)(4,1)S(1)}, s32[]{:S(2)}) async-start(s8[14680064]{0:T(1024)(128)(4,1)} %bitcast.121), calls=%async_computation.9 | async-start | bytes 8388608
  307.1 9.9 %slice-start.2 = ((s8[14680064]{0:T(1024)(128)(4,1)}), s8[4194304]{0:T(1024)(128)(4,1)S(1)}, s32[]{:S(2)}) async-start(s8[14680064]{0:T(1024)(128)(4,1)} %bitcast.121), calls=%async_computation.10 | async-start | bytes 8388608
  307.1 9.9 %slice-start.3 = ((s8[14680064]{0:T(1024)(128)(4,1)}), s8[2097152]{0:T(1024)(128)(4,1)S(1)}, s32[]{:S(2)}) async-start(s8[14680064]{0:T(1024)(128)(4,1)} %bitcast.121), calls=%async_computation.11 | async-start | bytes 4194304
  339.6 9.1 %copy-start.8 = (f32[32,2]{0,1:T(2,128)S(1)}, f32[32,2]{0,1:T(2,128)}, u32[]{:S(2)}) copy-start(f32[32,2]{0,1:T(2,128)} %param.33) | copy-start | bytes 772
  342.8 43.2 %all-to-all-start.1 = ((bf16[8,18,4096]{2,1,0:T(8,128)(2,1)}), bf16[8,18,4096]{2,1,0:T(8,128)(2,1)S(1)}, u32[]{:S(2)}, u32[]{:S(2)}) async-start(bf16[8,18,4096]{2,1,0:T(8,128)(2,1)} %copy.80), calls=%async_computation.2 | async-start | bytes 3145728 | tf_op jit(solution)/shard_map/all_to_all | solution.py:191
  348.7 37.6 %copy-start.1 = (bf16[64,4096]{1,0:T(8,128)(2,1)S(1)}, bf16[64,4096]{1,0:T(8,128)(2,1)}, u32[]{:S(2)}) copy-start(bf16[64,4096]{1,0:T(8,128)(2,1)} %copy-done) | copy-start | bytes 1572868
  348.7 37.6 %copy-start.3 = (f32[64,4096]{1,0:T(8,128)S(1)}, f32[64,4096]{1,0:T(8,128)}, u32[]{:S(2)}) copy-start(f32[64,4096]{1,0:T(8,128)} %all-reduce.2.cloned.1.call-done) | copy-start | bytes 3145732
Sparse Core Ops, SparseCore 0:
  10.1 75.5 all-gather.4
  87.7 123.4 all-gather.6
  217.4 17.5 all-reduce.1
  282.8 9.9 all-gather.8
  328.3 11.2 reduce-scatter.1
where the time goes:
time: 395 us; the launch traced here: 394 us
  waiting for transfers between devices  251 us (64%)
  blocking collectives  45.5 us (12%)
  matrix products  39.9 us (10%)
  local copies, waits for them, and re-layouts  31.2 us (8%)
  between operations  14.8 us (4%)
  starting transfers between devices  6.27 us (2%)
  other arithmetic  5.95 us (2%)
    all_gather x1, waiting for transfers between devices, shards(): weight_piece = lax.all_gather(wo, 'tok', axis=2, tiled=True)  105 us
    all_gather x1, waiting for transfers between devices, shards(): weight_piece = lax.all_gather(wkv, 'tok', axis=0, tiled=True)  69.3 us
    all_to_all x1, blocking collectives, shards(): lax.all_to_all(send_chip, 'tok', split_axis=0, concat_axis=0, tiled=True)  43 us
    all_to_all x1, waiting for transfers between devices, shards(): lax.all_to_all(chip_total[:, 0].astype(jnp.bfloat16), 'tok', split_axis=0...  36.6 us
    psum x1, waiting for transfers between devices, shards(): summed_heads = lax.psum(attn_out, 'mdl')  17.4 us
    reduce_scatter x1, waiting for transfers between devices, shards(): lax.psum_scatter(per_core.astype(jnp.bfloat16), 'mdl', scatter_dimension=...  11.4 us
    reshape x1, local copies, waits for them, and re-layouts, shards(): weight_piece.reshape(weight_piece.shape[0], -1)  11.3 us
    all_gather x1, waiting for transfers between devices, shards(): both_cores = lax.all_gather(received[:, None], 'mdl', axis=1, tiled=True)  9.91 us
  transfers between devices with their start and end apart: 6, of which 6 were waited for; matrix products, arithmetic and copies ran while one was open for 7% of the time, Pallas kernels for 0%

commit v1 on v0

--- a/solution.py
+++ b/solution.py
@@ -9,6 +9,29 @@
 eps_norm = 1e-05
 rope_base = 1000000.0
 mask_fill = -1e30
+
+
+def in_blocks(x, dim, size):
+    shape = x.shape
+    tiles = x.reshape(*shape[:dim], size, shape[dim] // size, *shape[dim + 1 :])
+    return jnp.moveaxis(tiles, dim, 0)
+
+
+def joined_along(tiles, dim):
+    tiles = jnp.moveaxis(tiles, 0, dim)
+    shape = tiles.shape
+    return tiles.reshape(*shape[:dim], shape[dim] * shape[dim + 1], *shape[dim + 2 :])
+
+
+def exchange_directly(x, axis, split_dim, concat_dim):
+    peers, index = (lax.axis_size(axis), lax.axis_index(axis))
+    blocks = in_blocks(x, split_dim, peers)
+    outs = [blocks[index]]
+    for hop in range(1, peers):
+        sent = blocks[(index + hop) % peers]
+        outs.append(lax.ppermute(sent, axis, [(i, (i + hop) % peers) for i in range(peers)]))
+    blocks = jnp.stack(outs)[(index - jnp.arange(peers)) % peers]
+    return joined_along(blocks, concat_dim)
 
 
 def rms_scale(values_in, gain):
@@ -171,7 +194,7 @@
     model_width = moe_in.shape[1]
     core_count = lax.axis_size("mdl")
     send_chip = jnp.repeat(send_rows, slabs // core_count, axis=0)
-    received = lax.all_to_all(send_chip, "tok", split_axis=0, concat_axis=0, tiled=True)
+    received = exchange_directly(send_chip, "tok", 0, 0)
     chip_count = received.shape[0]
     item_count = received.shape[1]
     both_cores = lax.all_gather(received[:, None], "mdl", axis=1, tiled=True)

time: 395 us -> 393 us (level)
  blocking collectives: 45.5 us -> 2.51 us
  waiting for transfers between devices: 251 us -> 276 us
  starting transfers between devices: 6.27 us -> 21.3 us
    all_to_all x1 -> x0, blocking collectives: 43 us -> none  [shards(): lax.all_to_all(send_chip, 'tok', split_axis=0, concat_axis=0, tiled=True)]
    ppermute x0 -> x7, starting transfers between devices: none -> 14.9 us  [exchange_directly(): lax.ppermute(sent, axis, [(i, (i + hop) % peers) for i in range(peers)])]
    ppermute x0 -> x7, waiting for transfers between devices: none -> 13.7 us  [exchange_directly(): lax.ppermute(sent, axis, [(i, (i + hop) % peers) for i in range(peers)])]
    all_gather x1, waiting for transfers between devices: 9.91 us -> 21.2 us  [shards(): both_cores = lax.all_gather(received[:, None], 'mdl', axis=1, tiled=True)]
  transfers between devices with their start and end apart: 6 -> 13, of which waited for: 6 -> 10; matrix products, arithmetic and copies ran while one was open for 7% -> 7% of each run, Pallas kernels for 0% -> 0%
where the time goes in v1:
time: 393 us
  waiting for transfers between devices  276 us (70%)
  matrix products  40 us (10%)
  local copies, waits for them, and re-layouts  32 us (8%)
  starting transfers between devices  21.3 us (5%)
  between operations  15 us (4%)
  other arithmetic  5.97 us (2%)
    all_gather x1, waiting for transfers between devices, shards(): weight_piece = lax.all_gather(wo, 'tok', axis=2, tiled=True)  105 us
    all_gather x1, waiting for transfers between devices, shards(): weight_piece = lax.all_gather(wkv, 'tok', axis=0, tiled=True)  69.3 us
    all_to_all x1, waiting for transfers between devices, shards(): lax.all_to_all(chip_total[:, 0].astype(jnp.bfloat16), 'tok', split_axis=0...  36.5 us
    all_gather x1, waiting for transfers between devices, shards(): both_cores = lax.all_gather(received[:, None], 'mdl', axis=1, tiled=True)  21.2 us
    psum x1, waiting for transfers between devices, shards(): summed_heads = lax.psum(attn_out, 'mdl')  17.3 us
    ppermute x7, starting transfers between devices, exchange_directly(): lax.ppermute(sent, axis, [(i, (i + hop) % peers) for i in range(peers)])  14.9 us
    ppermute x7, waiting for transfers between devices, exchange_directly(): lax.ppermute(sent, axis, [(i, (i + hop) % peers) for i in range(peers)])  13.7 us
    reduce_scatter x1, waiting for transfers between devices, shards(): lax.psum_scatter(per_core.astype(jnp.bfloat16), 'mdl', scatter_dimension=...  11.4 us
  transfers between devices with their start and end apart: 13, of which 10 were waited for; matrix products, arithmetic and copies ran while one was open for 7% of the time, Pallas kernels for 0%

profile of v1, /device:TPU:0, one launch (start us, length us, event | category | flops | bytes accessed | tf_op | source)
XLA Modules:
  0.0 392.5 jit_solution(2663439734765282250)
XLA Ops:
  7.2 0.7 all-gather.5.cloned.1.call-update
  8.0 0.7 all-gather.7.cloned.1.call-update
  9.4 0.7 convert_element_type.71
  10.1 2.5 all_gather.12
  12.6 0.2 fusion.73
  12.8 0.2 multiply_cosine_fusion
  13.1 3.0 fusion.117
  16.2 0.1 copy_bitcast_fusion
  16.4 69.3 %all-gather.5.cloned.1.call-done = bf16[4096,2,2,128]{3,2,1,0:T(2,128)(2,1)} async-done(((bf16[512,2,2,128]{3,2,1,0:T(2,128)(2,1)}), bf16[4096,2,2,128]{3,2,1,0:T(2,128)(2,1)}) %all-gather.5.cloned.1.call-update) | async-done | bytes 4194320 | tf_op jit(solution)/shard_map/all_gather | solution.py:138
  85.7 11.3 %copy.98 = bf16[4096,2,2,128]{0,3,2,1:T(8,128)(2,1)} copy(bf16[4096,2,2,128]{3,2,1,0:T(2,128)(2,1)} %all-gather.5.cloned.1.call-done) | data formatting | bytes 8388608 | tf_op jit(solution)/shard_map/reshape | solution.py:141
  96.9 3.7 fusion.121
  100.8 0.2 fusion.120
  101.0 0.2 fusion.119
  101.2 1.1 while.44
  101.2 0.7 add_compare_fusion.8
  101.9 0.3 fusion.146
  102.2 0.2 select_reduce_fusion.7
  102.4 0.2 fusion.92
  102.6 1.2 while.45
  102.6 0.7 add_compare_fusion.9
  103.3 0.5 fusion.150
  103.9 1.1 while.46
  103.9 0.7 add_compare_fusion.10
  104.6 0.3 fusion.152
  104.9 0.2 select_reduce_fusion.8
  105.1 0.2 fusion.93
  105.3 1.2 while.47
  105.3 0.7 add_compare_fusion.11
  105.9 0.5 fusion.156
  106.6 104.6 %all-gather.7.cloned.1.call-done = bf16[8,128,4096]{2,1,0:T(8,128)(2,1)} async-done(((bf16[8,128,512]{2,1,0:T(8,128)(2,1)}), bf16[8,128,4096]{2,1,0:T(8,128)(2,1)}) %all-gather.7.cloned.1.call-update) | async-done | bytes 8388624 | tf_op jit(solution)/shard_map/all_gather | solution.py:166
  211.2 6.1 %fusion.84 = f32[64,4096]{1,0:T(8,128)} fusion(bf16[1024,4096]{1,0:T(8,128)(2,1)} %bitcast.144, bf16[64,512]{1,0:T(8,128)(2,1)S(1)} %reshape.210, bf16[64,512]{1,0:T(8,128)(2,1)S(1)} %reshape.208), kind=kOutput, calls=%fused_computation.114 | convolution fusion | flops 537133056 | bytes 9568256 | tf_op jit(solution)/shard_map/dot_general | solution.py:167
  217.8 17.3 %all-reduce.2.cloned.1.call-done = f32[64,4096]{1,0:T(8,128)} async-done(((f32[64,4096]{1,0:T(8,128)}), f32[64,4096]{1,0:T(8,128)}) %all-reduce.2.cloned.1.call-update) | async-done | bytes 1048592 | tf_op jit(solution)/shard_map/psum | solution.py:174
  235.1 1.2 multiply_reduce_fusion
  236.3 1.5 convolution_convert_fusion
  237.8 0.2 broadcast_in_dim.138
  238.1 1.8 collective-permute-start
  240.0 1.5 collective-permute-start.1
  241.5 2.4 collective-permute-start.2
  243.9 1.4 collective-permute-start.3
  245.3 2.4 collective-permute-start.4
  247.7 1.1 collective-permute-done
  248.8 1.6 collective-permute-start.5
  250.5 3.7 collective-permute-start.6
  254.2 10.8 %collective-permute-done.2 = bf16[1,18,4096]{2,1,0:T(8,128)(2,1)S(1)} collective-permute-done((bf16[1,18,4096]{2,1,0:T(8,128)(2,1)S(1)}, bf16[1,18,4096]{2,1,0:T(8,128)(2,1)S(1)}, u32[]{:S(2)}, u32[]{:S(2)}) %collective-permute-start.2) | collective-permute-done | bytes 147488 | tf_op jit(solution)/shard_map/ppermute | solution.py:32
  265.0 0.5 collective-permute-done.3
  265.7 1.3 collective-permute-done.6
  266.9 0.6 gather_fusion
  267.6 1.7 copy.90
  269.3 0.2 reduce-scatter.2.cloned.1.call-start
  269.5 21.2 %all-gather.9.cloned.1.call-done = bf16[8,36,4096]{2,0,1:T(8,128)(2,1)} async-done(((bf16[8,18,4096]{2,0,1:T(8,128)(2,1)}), bf16[8,36,4096]{2,0,1:T(8,128)(2,1)}) %all-gather.9.cloned.1.call-update) | async-done | bytes 2359312 | tf_op jit(solution)/shard_map/all_gather | solution.py:200
  290.8 3.0 copy.91
  293.7 2.1 reshape_reshape.10
  295.9 9.1 %fusion.54 = f32[288,1792]{1,0:T(8,128)S(1)} fusion(bf16[288,4096]{1,0:T(8,128)(2,1)} %reshape_reshape.10, bf16[1,4096,1792]{2,1,0:T(8,128)(2,1)} %param.29), kind=kOutput, calls=%fused_computation.63 | convolution fusion | flops 4227858432 | bytes 19103744 | tf_op jit(solution)/shard_map/dot_general | solution.py:203
  305.0 9.9 %fusion.66 = bf16[288,1792]{1,0:T(8,128)(2,1)S(1)} fusion(bf16[288,4096]{1,0:T(8,128)(2,1)S(1)} %copy-done.4, bf16[1,4096,1792]{2,1,0:T(8,128)(2,1)} %param.30, f32[288,1792]{1,0:T(8,128)S(1)} %fusion.54), kind=kOutput, calls=%fused_computation.74 | convolution fusion | flops 4230955008 | bytes 20135936 | tf_op jit(solution)/shard_map/dot_general | solution.py:204
  314.9 5.8 %fusion.56 = bf16[288,4096]{1,0:T(8,128)(2,1)} fusion(bf16[288,1792]{1,0:T(8,128)(2,1)S(1)} %fusion.66, bf16[1,1792,4096]{2,1,0:T(8,128)(2,1)S(1)} %bitcast.154), kind=kOutput, calls=%fused_computation.65 | convolution fusion | flops 4229038080 | bytes 18071552 | tf_op jit(solution)/shard_map/dot_general | solution.py:206
  320.7 2.7 reshape_reshape.11
  323.4 2.7 copy.92
  326.2 11.4 %reduce-scatter.2.cloned.1.call-done = bf16[8,1,18,4096]{3,0,2,1:T(8,128)(2,1)} async-done(((bf16[8,2,18,4096]{3,0,2,1:T(8,128)(2,1)}), bf16[8,1,18,4096]{3,0,2,1:T(8,128)(2,1)}) %reduce-scatter.2.cloned.1.call-update) | async-done | bytes 1179664 | tf_op jit(solution)/shard_map/reduce_scatter | solution.py:211
  337.6 3.1 copy.93
  340.7 6.0 %all-to-all-start = ((bf16[8,18,4096]{2,1,0:T(8,128)(2,1)}), bf16[8,18,4096]{2,1,0:T(8,128)(2,1)S(1)}, u32[]{:S(2)}, u32[]{:S(2)}) async-start(bf16[8,18,4096]{2,1,0:T(8,128)(2,1)} %copy.93), calls=%async_computation.1 | async-start | bytes 3145728 | tf_op jit(solution)/shard_map/all_to_all | solution.py:214
  346.8 0.7 copy.96
  347.5 36.5 %all-to-all-done = bf16[8,18,4096]{2,1,0:T(8,128)(2,1)S(1)} async-done(((bf16[8,18,4096]{2,1,0:T(8,128)(2,1)}), bf16[8,18,4096]{2,1,0:T(8,128)(2,1)S(1)}, u32[]{:S(2)}, u32[]{:S(2)}) %all-to-all-start) | async-done | bytes 1179680 | tf_op jit(solution)/shard_map/all_to_all | solution.py:214
  384.1 0.3 convert_reduce_fusion
  384.4 1.6 fusion.60
  (78 shorter events, 1.4 us)
Async XLA Ops:
  7.2 5.9 %copy-start.5 = (bf16[64,8,128]{2,1,0:T(8,128)(2,1)S(1)}, bf16[64,8,128]{2,1,0:T(8,128)(2,1)}, u32[]{:S(2)}) copy-start(bf16[64,8,128]{2,1,0:T(8,128)(2,1)} %param.22) | copy-start | bytes 393220
  7.2 5.9 %copy-start.2 = (bf16[1,2048,2,2,128]{4,3,2,1,0:T(2,128)(2,1)S(1)}, bf16[1,2048,2,2,128]{4,3,2,1,0:T(2,128)(2,1)}, u32[]{:S(2)}) copy-start(bf16[1,2048,2,2,128]{4,3,2,1,0:T(2,128)(2,1)} %param.23) | copy-start | bytes 6291460
  7.2 78.5 %all-gather.5.cloned.1.call-start = ((), (), s32[]{:S(2)}) async-start(), calls=%async_computation.2 | async-start | bytes 4718592 | tf_op jit(solution)/shard_map/all_gather | solution.py:138
  7.9 203.3 %all-gather.7.cloned.1.call-start = ((), (), s32[]{:S(2)}) async-start(), calls=%async_computation.3 | async-start | bytes 9437184 | tf_op jit(solution)/shard_map/all_gather | solution.py:166
  8.7 226.4 %all-reduce.2.cloned.1.call-start = ((), (), s32[]{:S(2)}) async-start(), calls=%async_computation.4 | async-start | bytes 2097152 | tf_op jit(solution)/shard_map/psum | solution.py:174
  12.6 223.7 %copy-start = (bf16[64,4096]{1,0:T(8,128)(2,1)}, bf16[64,4096]{1,0:T(8,128)(2,1)S(1)}, u32[]{:S(2)}) copy-start(bf16[64,4096]{1,0:T(8,128)(2,1)S(1)} %all_gather.12) | copy-start | bytes 1572868
  211.2 6.3 %copy-start.7 = (s32[32,2]{0,1:T(2,128)S(1)}, s32[32,2]{0,1:T(2,128)}, u32[]{:S(2)}) copy-start(s32[32,2]{0,1:T(2,128)} %param.32) | copy-start | bytes 772
  211.2 6.5 %copy-start.6 = (bf16[4096]{0:T(1024)(128)(2,1)S(1)}, bf16[4096]{0:T(1024)(128)(2,1)}, u32[]{:S(2)}) copy-start(bf16[4096]{0:T(1024)(128)(2,1)} %param.28) | copy-start | bytes 24580
  217.3 73.4 %all-gather.9.cloned.1.call-start = ((), (), s32[]{:S(2)}) async-start(), calls=%async_computation.6 | async-start | bytes 3538944 | tf_op jit(solution)/shard_map/all_gather | solution.py:200
  238.1 10.7 %collective-permute-start = (bf16[1,18,4096]{2,1,0:T(8,128)(2,1)S(1)}, bf16[1,18,4096]{2,1,0:T(8,128)(2,1)S(1)}, u32[]{:S(2)}, u32[]{:S(2)}) collective-permute-start(bf16[1,18,4096]{2,1,0:T(8,128)(2,1)S(1)} %get-tuple-element.274), channel_id=1, source_target_pairs={{0,2},{2,4},{4,6},{6,8},{8,10},{10,12},{12,14},{14,0},{1,3},{3,5},... | collective-permute-start | bytes 442376 | tf_op jit(solution)/shard_map/ppermute | solution.py:32
  240.0 10.5 %collective-permute-start.1 = (bf16[1,18,4096]{2,1,0:T(8,128)(2,1)S(1)}, bf16[1,18,4096]{2,1,0:T(8,128)(2,1)S(1)}, u32[]{:S(2)}, u32[]{:S(2)}) collective-permute-start(bf16[1,18,4096]{2,1,0:T(8,128)(2,1)S(1)} %get-tuple-element.273), channel_id=1, source_target_pairs={{0,4},{2,6},{4,8},{6,10},{8,12},{10,14},{12,0},{14,2},{1,5},{3,7},... | collective-permute-start | bytes 442376 | tf_op jit(solution)/shard_map/ppermute | solution.py:32
  241.5 23.5 %collective-permute-start.2 = (bf16[1,18,4096]{2,1,0:T(8,128)(2,1)S(1)}, bf16[1,18,4096]{2,1,0:T(8,128)(2,1)S(1)}, u32[]{:S(2)}, u32[]{:S(2)}) collective-permute-start(bf16[1,18,4096]{2,1,0:T(8,128)(2,1)S(1)} %get-tuple-element.272), channel_id=1, source_target_pairs={{0,6},{2,8},{4,10},{6,12},{8,14},{10,0},{12,2},{14,4},{1,7},{3,9},... | collective-permute-start | bytes 442376 | tf_op jit(solution)/shard_map/ppermute | solution.py:32
  243.9 21.7 %collective-permute-start.3 = (bf16[1,18,4096]{2,1,0:T(8,128)(2,1)S(1)}, bf16[1,18,4096]{2,1,0:T(8,128)(2,1)S(1)}, u32[]{:S(2)}, u32[]{:S(2)}) collective-permute-start(bf16[1,18,4096]{2,1,0:T(8,128)(2,1)S(1)} %get-tuple-element.271), channel_id=1, source_target_pairs={{0,8},{2,10},{4,12},{6,14},{8,0},{10,2},{12,4},{14,6},{1,9},{3,11}... | collective-permute-start | bytes 442376 | tf_op jit(solution)/shard_map/ppermute | solution.py:32
  245.3 20.3 %collective-permute-start.4 = (bf16[1,18,4096]{2,1,0:T(8,128)(2,1)S(1)}, bf16[1,18,4096]{2,1,0:T(8,128)(2,1)S(1)}, u32[]{:S(2)}, u32[]{:S(2)}) collective-permute-start(bf16[1,18,4096]{2,1,0:T(8,128)(2,1)S(1)} %get-tuple-element.270), channel_id=1, source_target_pairs={{0,10},{2,12},{4,14},{6,0},{8,2},{10,4},{12,6},{14,8},{1,11},{3,13... | collective-permute-start | bytes 442376 | tf_op jit(solution)/shard_map/ppermute | solution.py:32
  248.8 16.8 %collective-permute-start.5 = (bf16[1,18,4096]{2,1,0:T(8,128)(2,1)S(1)}, bf16[1,18,4096]{2,1,0:T(8,128)(2,1)S(1)}, u32[]{:S(2)}, u32[]{:S(2)}) collective-permute-start(bf16[1,18,4096]{2,1,0:T(8,128)(2,1)S(1)} %get-tuple-element.269), channel_id=1, source_target_pairs={{0,12},{2,14},{4,0},{6,2},{8,4},{10,6},{12,8},{14,10},{1,13},{3,15... | collective-permute-start | bytes 442376 | tf_op jit(solution)/shard_map/ppermute | solution.py:32
  250.5 16.4 %collective-permute-start.6 = (bf16[1,18,4096]{2,1,0:T(8,128)(2,1)S(1)}, bf16[1,18,4096]{2,1,0:T(8,128)(2,1)S(1)}, u32[]{:S(2)}, u32[]{:S(2)}) collective-permute-start(bf16[1,18,4096]{2,1,0:T(8,128)(2,1)S(1)} %get-tuple-element.268), channel_id=1, source_target_pairs={{0,14},{2,0},{4,2},{6,4},{8,6},{10,8},{12,10},{14,12},{1,15},{3,1}... | collective-permute-start | bytes 442376 | tf_op jit(solution)/shard_map/ppermute | solution.py:32
  269.3 68.3 %reduce-scatter.2.cloned.1.call-start = ((), (), s32[]{:S(2)}) async-start(), calls=%async_computation.5 | async-start | bytes 3538944 | tf_op jit(solution)/shard_map/reduce_scatter | solution.py:211
  295.9 9.1 %copy-start.4 = (bf16[288,4096]{1,0:T(8,128)(2,1)S(1)}, bf16[288,4096]{1,0:T(8,128)(2,1)}, u32[]{:S(2)}) copy-start(bf16[288,4096]{1,0:T(8,128)(2,1)} %reshape_reshape.10) | copy-start | bytes 7077892
  295.9 19.0 %slice-start = ((s8[14680064]{0:T(1024)(128)(4,1)}), s8[4194304]{0:T(1024)(128)(4,1)S(1)}, s32[]{:S(2)}) async-start(s8[14680064]{0:T(1024)(128)(4,1)} %bitcast.153), calls=%async_computation.7 | async-start | bytes 8388608
  295.9 19.0 %slice-start.1 = ((s8[14680064]{0:T(1024)(128)(4,1)}), s8[4194304]{0:T(1024)(128)(4,1)S(1)}, s32[]{:S(2)}) async-start(s8[14680064]{0:T(1024)(128)(4,1)} %bitcast.153), calls=%async_computation.8 | async-start | bytes 8388608
  305.0 9.9 %slice-start.2 = ((s8[14680064]{0:T(1024)(128)(4,1)}), s8[4194304]{0:T(1024)(128)(4,1)S(1)}, s32[]{:S(2)}) async-start(s8[14680064]{0:T(1024)(128)(4,1)} %bitcast.153), calls=%async_computation.9 | async-start | bytes 8388608
  305.0 9.9 %slice-start.3 = ((s8[14680064]{0:T(1024)(128)(4,1)}), s8[2097152]{0:T(1024)(128)(4,1)S(1)}, s32[]{:S(2)}) async-start(s8[14680064]{0:T(1024)(128)(4,1)} %bitcast.153), calls=%async_computation.10 | async-start | bytes 4194304
  340.7 6.0 %copy-start.8 = (f32[32,2]{0,1:T(2,128)S(1)}, f32[32,2]{0,1:T(2,128)}, u32[]{:S(2)}) copy-start(f32[32,2]{0,1:T(2,128)} %param.33) | copy-start | bytes 772
  340.7 43.3 %all-to-all-start = ((bf16[8,18,4096]{2,1,0:T(8,128)(2,1)}), bf16[8,18,4096]{2,1,0:T(8,128)(2,1)S(1)}, u32[]{:S(2)}, u32[]{:S(2)}) async-start(bf16[8,18,4096]{2,1,0:T(8,128)(2,1)} %copy.93), calls=%async_computation.1 | async-start | bytes 3145728 | tf_op jit(solution)/shard_map/all_to_all | solution.py:214
  346.8 37.6 %copy-start.1 = (bf16[64,4096]{1,0:T(8,128)(2,1)S(1)}, bf16[64,4096]{1,0:T(8,128)(2,1)}, u32[]{:S(2)}) copy-start(bf16[64,4096]{1,0:T(8,128)(2,1)} %copy-done) | copy-start | bytes 1572868
  346.8 37.6 %copy-start.3 = (f32[64,4096]{1,0:T(8,128)S(1)}, f32[64,4096]{1,0:T(8,128)}, u32[]{:S(2)}) copy-start(f32[64,4096]{1,0:T(8,128)} %all-reduce.2.cloned.1.call-done) | copy-start | bytes 3145732
Sparse Core Ops, SparseCore 0:
  10.1 75.5 all-gather.4
  87.7 123.4 all-gather.6
  217.5 17.5 all-reduce.1
  269.4 21.2 all-gather.8
  326.3 11.2 reduce-scatter.1
